TPU v7x, 32 devices: a whole 2x2x4 slice. The times are simulated.
32 devices in a mesh: row: 8 (over z, x), col: 4 (over y, core).
Axes of the slice: x: 2, y: 2, z: 4, core: 2. Of those that a mesh axis runs over, the one named last changes fastest.
Arguments:
- tile_values: bfloat16 [192, 512, 128], P('row', 'col'), may hold values from -0.0546875 to 0.0546875
- tile_counts: int32 [96, 4], P('row', 'col'), may hold values from 0 to 2, as said below
- tile_cols: int32 [192, 4], P('row', 'col'), may hold values from 0 to 1, as said below
- panels: bfloat16 [12288, 4096], P('row', 'col'), may hold values from -6 to 6
Outputs:
- product: bfloat16 [1024, 4096], P('col', 'row')
Inputs may be any that keep to these rules, and one draw needn't show every extreme that they name: `tile_counts`: within each device the filled slots follow block row order; a device holds at most 24 tiles and some device holds exactly 24 in every draw. `tile_cols`: within one block row of a device the filled slots' columns rise strictly; entries of unfilled slots carry no meaning.
All inputs are finite; a program needn't handle non-finite values.
Results may differ from a plain program's by a relative error of at most 0.001.
Values may be sent and summed in bfloat16 or wider, within the bound.
No kernel may reach another device: no remote copies, remote signals or barrier semaphores. Data moves between devices by JAX's collectives and lax.ppermute only.
A program may use at most 64 MiB of HBM per device.

v0:
```python
import functools

import jax
import jax.numpy as jnp
from jax import lax
from jax.experimental import pallas as pl
from jax.experimental.pallas import tpu as pltpu
from jax.sharding import PartitionSpec as P


GROUPS = 1
SUB = 8
TOP = 32767.0
STEPS = 128.0
VMEM = pl.BlockSpec(memory_space=pltpu.VMEM)
SMALL = pltpu.CompilerParams(vmem_limit_bytes=16 * 2**20)


def encode(value, ref, at=slice(None)):
    height, width = value.shape
    part = height // GROUPS
    for g in range(GROUPS):
        rows = value[g * part : (g + 1) * part].reshape(part // SUB, SUB, width)
        largest = jnp.max(jnp.abs(rows), axis=0)
        code = jnp.ceil(jnp.log2(jnp.maximum(largest, 1e-30)) * STEPS)
        factor = TOP / jnp.exp2(code / STEPS)
        whole = jnp.clip(jnp.round(rows * factor[None]), -TOP, TOP).astype(jnp.int32)
        ref[g * part : (g + 1) * part, at] = whole.reshape(part, width).astype(jnp.int16)
        whole = code.astype(jnp.int32)
        code_rows = whole if g == 0 else jnp.concatenate([code_rows, whole], 0)
    ref[height : height + GROUPS * SUB, at] = code_rows.astype(jnp.int16)


def decode(coded, height):
    width = coded.shape[1]
    part = height // GROUPS
    codes = coded[height : height + GROUPS * SUB].astype(jnp.int32).astype(jnp.float32)
    pieces = []
    for g in range(GROUPS):
        scale = jnp.exp2(codes[g * SUB : (g + 1) * SUB] / STEPS) * (1.0 / TOP)
        rows = coded[g * part : (g + 1) * part].astype(jnp.int32).astype(jnp.float32)
        pieces.append((rows.reshape(part // SUB, SUB, width) * scale[None]).reshape(part, width))
    return jnp.concatenate(pieces, 0)


def places(spread):
    r, c = lax.axis_index("row"), lax.axis_index("col")
    q = r // spread
    return r % spread, (q + c) % 2, (q // 2) ^ (c // 2)


def near_memory(value):
    return pltpu.with_memory_space_constraint(value, pltpu.VMEM)


def far_memory(value):
    return pltpu.with_memory_space_constraint(value, pltpu.HBM)


FIRST = {"a": "x", "b": "z", "0": "xz", "1": "xz"}
OWN = ("a", "b")
PARTS = (144, 112)
TURN = ("0",)
PLAN = (
    "leave_a",
    "first_a",
    "leave_b",
    "first_b",
    "stay_a",
    "stay_b",
    "leave_0",
    "first_0",
    "split_a",
    "second_a",
    "split_b",
    "second_b",
    "stay_0",
    "leave_1",
    "first_1",
    "stay_1",
    "code_0",
    "near_0",
    "code_a",
    "far_a",
    "code_b",
    "far_b",
    "far_0",
    "code_1",
    "near_1",
    "far_1",
)
KERNELS = ("leave", "stay", "split", "code")


def build_kernel(counts_in, columns_in, tiles_in, panels_in, *refs):
    outs, (panels, counts, columns, tiles, sems) = refs[:-5], refs[-5:]
    copies = [
        pltpu.make_async_copy(source, target, sems.at[k])
        for k, (source, target) in enumerate(
            ((counts_in, counts), (columns_in, columns), (tiles_in, tiles), (panels_in, panels))
        )
    ]
    for copy in copies:
        copy.start()
    for copy in copies[:-1]:
        copy.wait()
    tall, slots = counts.shape[0], tiles.shape[0]
    wide = slots // tall
    edge = tiles.shape[1]
    start = jnp.int32(0)
    for i in range(tall):
        count = counts[i]
        for j in range(wide):
            slot, found = jnp.int32(0), jnp.int32(0)
            for t in range(wide):
                at = jnp.minimum(start + t, slots - 1)
                hit = (t < count) & (columns[at] == j)
                slot = jnp.where(hit, at, slot)
                found = jnp.where(hit, 1, found)
            tile = tiles[slot].astype(jnp.float32) * found.astype(jnp.float32)
            tile = tile.T.astype(jnp.bfloat16)
            at = slice(i * edge, (i + 1) * edge)
            outs[j][:, at] = tile
            top = 0
            for out in outs[wide:]:
                low, high = max(top, j * edge), min(top + out.shape[0], (j + 1) * edge)
                if low < high:
                    out[low - top : high - top, at] = tile[low - j * edge : high - j * edge]
                top += out.shape[0]
        start = start + count
    copies[-1].wait()


def build(tile_values, tile_counts, tile_cols, panels):
    slots, edge, _ = tile_values.shape
    tall = tile_counts.shape[0]
    wide = slots // tall
    heights = [edge] * wide + [part * edge // 128 for part in PARTS]
    return pl.pallas_call(
        build_kernel,
        out_shape=[jax.ShapeDtypeStruct((height, tall * edge), jnp.bfloat16) for height in heights]
        + [jax.ShapeDtypeStruct(panels.shape, panels.dtype)],
        in_specs=[pl.BlockSpec(memory_space=pltpu.HBM)] * 4,
        out_specs=[VMEM] * (len(heights) + 1),
        scratch_shapes=[
            pltpu.SMEM((tall,), jnp.int32),
            pltpu.SMEM((slots,), jnp.int32),
            pltpu.VMEM(tile_values.shape, tile_values.dtype),
            pltpu.SemaphoreType.DMA((4,)),
        ],
        compiler_params=SMALL,
        name="build",
    )(far_memory(tile_counts[:, 0]), far_memory(tile_cols[:, 0]), far_memory(tile_values), far_memory(panels))


def product_kernel(*refs, count, coded, spread):
    blocks, panels, out = refs[:count], refs[count:-1], refs[-1]
    a = jnp.concatenate([b[...] for b in blocks], 0) if count > 1 else blocks[0][...]
    half = out.shape[1]
    step = min(half, 256)
    side = places(spread)[0]
    start = (1 - side if coded else side) * half
    for n in range(0, half, step):
        at = pl.multiple_of(start + n, step)
        value = jnp.concatenate(
            [jnp.dot(a, b[:, pl.ds(at, step)], preferred_element_type=jnp.float32) for b in panels], 0
        )
        if coded:
            encode(value, out, slice(n, n + step))
        else:
            out[:, n : n + step] = value


def products(blocks, panels, half, coded):
    height = len(panels) * len(blocks) * blocks[0].shape[0]
    if coded:
        shape = jax.ShapeDtypeStruct((height + GROUPS * SUB, half), jnp.int16)
    else:
        shape = jax.ShapeDtypeStruct((height, half), jnp.float32)
    return pl.pallas_call(
        functools.partial(
            product_kernel, count=len(blocks), coded=coded, spread=panels[0].shape[1] // half
        ),
        out_shape=shape,
        in_specs=[VMEM] * (len(blocks) + len(panels)),
        out_specs=VMEM,
        compiler_params=SMALL,
        name="leaving" if coded else "staying",
    )(*blocks, *panels)


def coded_shape(height, half):
    return jax.ShapeDtypeStruct((height + GROUPS * SUB, half), jnp.int16)


def split_kernel(*refs, spread):
    codeds, kept, hold, send = refs[:-3], refs[-3], refs[-2], refs[-1]
    height = kept.shape[0] // 2
    each = kept.shape[0] // len(codeds)
    value = kept[...] + jnp.concatenate([decode(coded[...], each) for coded in codeds], 0)
    first, second = value[:height], value[height:]
    stays = places(spread)[1] == 0
    hold[...] = jnp.where(stays, first, second)
    encode(jnp.where(stays, second, first), send)


def split(codeds, kept, spread):
    height, half = kept.shape[0] // 2, kept.shape[1]
    return pl.pallas_call(
        functools.partial(split_kernel, spread=spread),
        out_shape=[jax.ShapeDtypeStruct((height, half), jnp.float32), coded_shape(height, half)],
        in_specs=[VMEM] * (len(codeds) + 1),
        out_specs=[VMEM, VMEM],
        compiler_params=SMALL,
        name="split",
    )(*codeds, kept)


def merge_kernel(*refs, count):
    codeds, kept, outs = refs[:count], refs[count], refs[count + 1 :]
    value = kept[...]
    for coded in codeds:
        value = value + decode(coded[...], kept.shape[0])
    for hold in outs[:-1]:
        hold[...] = value
    encode(value, outs[-1])


def merge(codeds, kept, holds):
    height, half = kept.shape
    out = pl.pallas_call(
        functools.partial(merge_kernel, count=len(codeds)),
        out_shape=[jax.ShapeDtypeStruct((height, half), jnp.float32)] * holds + [coded_shape(height, half)],
        in_specs=[VMEM] * (len(codeds) + 1),
        out_specs=[VMEM] * (holds + 1),
        compiler_params=SMALL,
        name="merge",
    )(*codeds, kept)
    return out if holds else (None, out[0])


def finish_kernel(*refs, count, heights, spread):
    kepts, codeds = refs[:count], refs[count : 2 * count]
    parts, out = refs[2 * count : -1], refs[-1]
    pick = places(spread)[2]
    value = jnp.concatenate(
        [kept[...] + decode(coded[...], kept.shape[0]) for kept, coded in zip(kepts, codeds)], 0
    )
    chunks = len(heights)
    for k in range(len(parts) // (2 * chunks)):
        pieces = []
        for j, height in enumerate(heights):
            at = 2 * (k * chunks + j)
            pieces.append(decode(parts[at][...], height) + decode(parts[at + 1][...], height))
        value = jnp.where(pick == k + 1, jnp.concatenate(pieces, 0), value)
    out[...] = value.astype(jnp.bfloat16)


def finish(kepts, codeds, parts, heights, spread):
    return pl.pallas_call(
        functools.partial(finish_kernel, count=len(kepts), heights=heights, spread=spread),
        out_shape=jax.ShapeDtypeStruct((sum(heights), kepts[0].shape[1]), jnp.bfloat16),
        in_specs=[VMEM] * (2 * len(kepts) + len(parts)),
        out_specs=VMEM,
        compiler_params=SMALL,
        name="finish",
    )(*kepts, *codeds, *parts)


def chosen_kernel(block, *refs, coded, spread):
    panels, out = refs[:-1], refs[-1]
    width = out.shape[1]
    step = min(width, 256)
    stays = places(spread)[1]
    for k, panel in enumerate(panels):

        @pl.when(stays == (1 - k if coded else k))
        def _():
            for n in range(0, width, step):
                at = slice(n, n + step)
                value = jnp.dot(block[...], panel[:, at], preferred_element_type=jnp.float32)
                if coded:
                    encode(value, out, at)
                else:
                    out[:, at] = value


def chosen(block, panels, spread, coded):
    height, width = block.shape[0], panels[0].shape[1]
    return pl.pallas_call(
        functools.partial(chosen_kernel, coded=coded, spread=spread),
        out_shape=coded_shape(height, width) if coded else jax.ShapeDtypeStruct((height, width), jnp.float32),
        in_specs=[VMEM] * 3,
        out_specs=VMEM,
        compiler_params=SMALL,
        name="chosen",
    )(block, *panels)


def quarter_kernel(block, first, second, *outs, coded, spread):
    half = outs[0].shape[1]
    step = min(half, 256)
    side, stays, _ = places(spread)
    here, there = side * half, (1 - side) * half

    def write(panel, start, out):
        for n in range(0, half, step):
            at = pl.ds(pl.multiple_of(start + n, step), step)
            value = jnp.dot(block[...], panel[:, at], preferred_element_type=jnp.float32)
            if coded:
                encode(value, out, slice(n, n + step))
            else:
                out[:, n : n + step] = value

    for k, (kept, left) in enumerate(((first, second), (second, first))):

        @pl.when(stays == k)
        def _():
            if coded:
                write(kept, there, outs[0])
                write(left, here, outs[1])
                write(left, there, outs[2])
            else:
                write(kept, here, outs[0])


def quarters(block, panels, spread, coded):
    height, half = block.shape[0], panels[0].shape[1] // spread
    kept = [jax.ShapeDtypeStruct((height, half), jnp.float32)]
    out = pl.pallas_call(
        functools.partial(quarter_kernel, coded=coded, spread=spread),
        out_shape=[coded_shape(height, half)] * 3 if coded else kept,
        in_specs=[VMEM] * 3,
        out_specs=[VMEM] * (3 if coded else 1),
        compiler_params=SMALL,
        name="quarters",
    )(block, *panels)
    return out if coded else out[0]


def halve_kernel(coded, kept, hold, send, *, spread):
    height, half = hold.shape
    side = places(spread)[0]

    def value(which):
        at = pl.ds(pl.multiple_of(which * half, half), half)
        return kept[:, at] + decode(coded[:, at], height)

    encode(value(1 - side), send)
    hold[...] = value(side)


def halve(coded, kept, spread):
    height, half = kept.shape[0], kept.shape[1] // spread
    return pl.pallas_call(
        functools.partial(halve_kernel, spread=spread),
        out_shape=[jax.ShapeDtypeStruct((height, half), jnp.float32), coded_shape(height, half)],
        in_specs=[VMEM, VMEM],
        out_specs=[VMEM, VMEM],
        compiler_params=SMALL,
        name="halve",
    )(coded, kept)


def after(value, *others):
    return lax.optimization_barrier((value, *others))[0]


def solution(mesh):
    rows, cols = mesh.shape["row"], mesh.shape["col"]
    spread = rows // cols
    assert spread == 2 and rows & (rows - 1) == 0 and cols >= 4

    def permute(value, move):
        pairs = [
            (r * cols + c, to[0] * cols + to[1])
            for r in range(rows)
            for c in range(cols)
            if (to := move(r, c)) is not None
        ]
        return lax.ppermute(value, ("row", "col"), pairs)

    last = cols // 2

    last = cols // 2
    inner = last - 2

    def met(r, c, bits):
        return not ((r // spread) ^ c) & bits

    def across(value):
        return permute(value, lambda r, c: (r ^ 1, c))

    def along(value):
        return permute(value, lambda r, c: (r ^ spread, c))

    def diagonal(value):
        return permute(value, lambda r, c: (r ^ spread ^ 1, c))

    def folded(send, hold):
        bit = 2
        while bit < last:
            got = permute(
                send,
                lambda r, c: (r ^ (bit * spread), c) if met(r, c, bit - 2) and not met(r, c, bit) else None,
            )
            hold, send = merge([got], hold, 1)
            bit *= 2
        return hold, send

    def body(tile_values, tile_counts, tile_cols, panels):
        half = panels.shape[1] // spread
        other = near_memory(permute(panels, lambda r, c: (r, c ^ 1)))
        *own, panels = [near_memory(x) for x in build(tile_values, tile_counts, tile_cols, panels)]
        chunks = len(PARTS)
        own, dense = own[:-chunks], {0: own[-chunks:]}
        bit = last
        while bit > 1:
            for m in list(dense):
                blocks = []
                for j in range(chunks):
                    blocks.append(near_memory(permute(dense[m][j], lambda r, c: (r, c ^ bit))))
                dense[m ^ bit] = blocks
            bit //= 2
        moved = [m for m in sorted(dense) if m]

        both = [panels, other]
        block = {name: [value] for name, value in zip(OWN, own)}
        for j in range(chunks):
            block[f"{j}"] = [dense[m][j] for m in moved]
        done, order = {}, []

        def tied(value):
            return after(value, *order) if order else value

        def multiply(name, k, coded):
            value = tied(block[name][k])
            if FIRST[name] == "x":
                return products([value], both, half, coded)
            return (chosen if FIRST[name] == "z" else quarters)(value, both, spread, coded)

        def leave(name, k):
            return multiply(name, k, True)

        def stay(name, k):
            return multiply(name, k, False)

        def first(name, k):
            value = done["leave", name][k]
            if FIRST[name] == "xz":
                return [across(value[0]), along(value[1]), diagonal(value[2])]
            return (across if FIRST[name] == "x" else along)(value)

        def separate(name, k):
            got, kept = tied(done["first", name][k]), done["stay", name][k]
            return split([got], kept, spread) if FIRST[name] == "x" else halve(got, kept, spread)

        def second(name, k):
            return (along if FIRST[name] == "x" else across)(done["split", name][k][1])

        def code(name, k):
            if FIRST[name] == "xz":
                gots, hold = list(done["first", name][k]), done["stay", name][k]
            else:
                gots, hold = [done["second", name][k]], done["split", name][k][0]
            gots[0] = tied(gots[0])
            if inner or name in OWN:
                return folded(*reversed(merge(gots, hold, 1)))
            return merge(gots, hold, 0)

        def near(name, k):
            m, bits = moved[k], inner if name in TURN else inner | last
            return permute(
                done["code", name][k][1], lambda r, c: (r, c ^ m) if met(r, c, bits) else None
            )

        def far(name, k):
            shift = last * spread
            if name in OWN or name not in TURN:
                m = 0 if name in OWN else moved[k]
                return permute(
                    done["code", name][k][1],
                    lambda r, c: (r ^ shift, c ^ m) if met(r, c, inner) and not met(r, c, last) else None,
                )
            m = moved[k]
            return permute(
                done["near", name][k],
                lambda r, c: (r ^ shift, c) if met(r, c ^ m, inner) and not met(r, c ^ m, last) else None,
            )

        actions = dict(leave=leave, stay=stay, first=first, split=separate, second=second, code=code, near=near, far=far)
        for step in PLAN:
            kind, name = step.split("_")
            results = []
            for k in range(len(block.get(name, (0,)))):
                results.append(actions[kind](name, k))
                if kind in KERNELS:
                    value = results[-1]
                    order = [value[-1] if isinstance(value, (tuple, list)) else value]
            done[kind, name] = results

        parts = []
        for k in range(len(moved)):
            for j in range(chunks):
                parts += [done["near", f"{j}"][k], done["far", f"{j}"][k]]
        kepts = [done["code", name][0][0] for name in OWN]
        heights = tuple(value.shape[0] for value in dense[0])
        return finish(kepts, [done["far", name][0] for name in OWN], parts, heights, spread)

    return jax.shard_map(
        body,
        mesh=mesh,
        in_specs=(P("row", "col", None), P("row", "col"), P("row", "col"), P("row", "col")),
        out_specs=P("col", "row"),
        check_vma=False,
    )
```

profile of v0, /device:TPU:0, one launch (start us, length us, event | category | flops | bytes accessed | tf_op | source)
XLA Modules:
  0.0 57.4 jit_solution(8013977574707008297)
XLA Ops:
  0.5 2.2 %build.1 = (bf16[128,1536]{1,0:T(8,128)(2,1)S(1)}, bf16[128,1536]{1,0:T(8,128)(2,1)S(1)}, bf16[144,1536]{1,0:T(8,128)(2,1)S(1)}, bf16[112,1536]{1,0:T(8,128)(2,1)S(1)}, bf16[1536,1024]{1,0:T(8,128)(2,1)S(1)}) custom-call(s32[12]{0:T(128)} %bitcast.2, s32[24]{0:T(128)} %bitcast.3, bf16[24,128,128]{2,1,0:T(8,128)(2,1)} %tiles_in.1, bf16[1536,1024]{1,0:T(8,128)(2,1)} %panels_in.1), custom_call_target="tpu_custom_call" | custom-call | tf_op jit(solution)/shard_map/build/pallas_call | solution.py:139
  2.7 2.6 %collective-permute-start.2 = (bf16[144,1536]{1,0:T(8,128)(2,1)S(1)}, bf16[144,1536]{1,0:T(8,128)(2,1)S(1)}, u32[]{:S(2)}, u32[]{:S(2)}) collective-permute-start(bf16[144,1536]{1,0:T(8,128)(2,1)S(1)} %get-tuple-element.39), channel_id=1, source_target_pairs={{0,2},{1,3},{2,0},{3,1},{4,6},{5,7},{6,4},{7,5},{8,10},{9,11},{10,... | collective-permute-start | bytes 1327112 | tf_op jit(solution)/shard_map/ppermute | solution.py:381
  6.8 2.9 %collective-permute-start.1 = (s16[264,512]{1,0:T(8,128)(2,1)S(1)}, s16[264,512]{1,0:T(8,128)(2,1)S(1)}, u32[]{:S(2)}, u32[]{:S(2)}) collective-permute-start(s16[264,512]{1,0:T(8,128)(2,1)S(1)} %leaving.1), channel_id=1, source_target_pairs={{0,4},{1,5},{2,6},{3,7},{4,0},{5,1},{6,2},{7,3},{8,12},{9,13},{10,... | collective-permute-start | bytes 811016 | tf_op jit(solution)/shard_map/ppermute | solution.py:381
  10.4 1.6 %collective-permute-start.6 = (s16[136,1024]{1,0:T(8,128)(2,1)S(1)}, s16[136,1024]{1,0:T(8,128)(2,1)S(1)}, u32[]{:S(2)}, u32[]{:S(2)}) collective-permute-start(s16[136,1024]{1,0:T(8,128)(2,1)S(1)} %chosen.2), channel_id=1, source_target_pairs={{0,8},{1,9},{2,10},{3,11},{4,12},{5,13},{6,14},{7,15},{8,0},{9,1},... | collective-permute-start | bytes 835592 | tf_op jit(solution)/shard_map/ppermute | solution.py:381
  12.0 1.5 %collective-permute-start.5 = (bf16[112,1536]{1,0:T(8,128)(2,1)S(1)}, bf16[112,1536]{1,0:T(8,128)(2,1)S(1)}, u32[]{:S(2)}, u32[]{:S(2)}) collective-permute-start(bf16[112,1536]{1,0:T(8,128)(2,1)S(1)} %get-tuple-element.49), channel_id=1, source_target_pairs={{0,2},{1,3},{2,0},{3,1},{4,6},{5,7},{6,4},{7,5},{8,10},{9,11},{10,... | collective-permute-start | bytes 1032200 | tf_op jit(solution)/shard_map/ppermute | solution.py:381
  14.8 1.5 %collective-permute-done.2.block = bf16[144,1536]{1,0:T(8,128)(2,1)S(1)} collective-permute-done((bf16[144,1536]{1,0:T(8,128)(2,1)S(1)}, bf16[144,1536]{1,0:T(8,128)(2,1)S(1)}, u32[]{:S(2)}, u32[]{:S(2)}) %collective-permute-start.2) | collective-permute-done | bytes 442400 | tf_op jit(solution)/shard_map/ppermute | solution.py:381
  16.3 1.0 %quarters.4 = (s16[152,512]{1,0:T(8,128)(2,1)S(1)}, s16[152,512]{1,0:T(8,128)(2,1)S(1)}, s16[152,512]{1,0:T(8,128)(2,1)S(1)}) custom-call(bf16[144,1536]{1,0:T(8,128)(2,1)S(1)} %collective-permute-done.2.block, bf16[1536,1024]{1,0:T(8,128)(2,1)S(1)} %get-tuple-element.38.refs_1_.refs_0_.first, bf16[1536,1024]{1,0:T(8,128)(2,1)S(1)} %collective-permute-done.refs_2_.refs_1_.second), custom_call_target="tpu_custom_call" | custom-call | tf_op jit(solution)/shard_map/quarters/pallas_call | solution.py:330
  17.3 2.1 %collective-permute-start.4 = (s16[152,512]{1,0:T(8,128)(2,1)S(1)}, s16[152,512]{1,0:T(8,128)(2,1)S(1)}, u32[]{:S(2)}, u32[]{:S(2)}) collective-permute-start(s16[152,512]{1,0:T(8,128)(2,1)S(1)} %get-tuple-element.48), channel_id=1, source_target_pairs={{0,4},{1,5},{2,6},{3,7},{4,0},{5,1},{6,2},{7,3},{8,12},{9,13},{10,... | collective-permute-start | bytes 466952 | tf_op jit(solution)/shard_map/ppermute | solution.py:381
  19.4 1.6 %collective-permute-start.7 = (s16[152,512]{1,0:T(8,128)(2,1)S(1)}, s16[152,512]{1,0:T(8,128)(2,1)S(1)}, u32[]{:S(2)}, u32[]{:S(2)}) collective-permute-start(s16[152,512]{1,0:T(8,128)(2,1)S(1)} %get-tuple-element.57), channel_id=1, source_target_pairs={{0,8},{1,9},{2,10},{3,11},{4,12},{5,13},{6,14},{7,15},{8,0},{9,1},... | collective-permute-start | bytes 466952 | tf_op jit(solution)/shard_map/ppermute | solution.py:381
  21.1 2.1 %collective-permute-start.3 = (s16[136,512]{1,0:T(8,128)(2,1)S(1)}, s16[136,512]{1,0:T(8,128)(2,1)S(1)}, u32[]{:S(2)}, u32[]{:S(2)}) collective-permute-start(s16[136,512]{1,0:T(8,128)(2,1)S(1)} %get-tuple-element.47), channel_id=1, source_target_pairs={{0,8},{1,9},{2,10},{3,11},{4,12},{5,13},{6,14},{7,15},{8,0},{9,1},... | collective-permute-start | bytes 417800 | tf_op jit(solution)/shard_map/ppermute | solution.py:381
  23.8 1.0 %quarters.6 = (s16[120,512]{1,0:T(8,128)(2,1)S(1)}, s16[120,512]{1,0:T(8,128)(2,1)S(1)}, s16[120,512]{1,0:T(8,128)(2,1)S(1)}) custom-call(bf16[112,1536]{1,0:T(8,128)(2,1)S(1)} %collective-permute-done.5.block, bf16[1536,1024]{1,0:T(8,128)(2,1)S(1)} %get-tuple-element.38.refs_1_.refs_0_.first, bf16[1536,1024]{1,0:T(8,128)(2,1)S(1)} %collective-permute-done.refs_2_.refs_1_.second), custom_call_target="tpu_custom_call" | custom-call | tf_op jit(solution)/shard_map/quarters/pallas_call | solution.py:330
  25.3 1.0 %collective-permute-done.7.refs_1_ = s16[152,512]{1,0:T(8,128)(2,1)S(1)} collective-permute-done((s16[152,512]{1,0:T(8,128)(2,1)S(1)}, s16[152,512]{1,0:T(8,128)(2,1)S(1)}, u32[]{:S(2)}, u32[]{:S(2)}) %collective-permute-start.7) | collective-permute-done | bytes 155680 | tf_op jit(solution)/shard_map/ppermute | solution.py:381
  26.3 2.5 %collective-permute-done.8.refs_2_ = s16[152,512]{1,0:T(8,128)(2,1)S(1)} collective-permute-done((s16[152,512]{1,0:T(8,128)(2,1)S(1)}, s16[152,512]{1,0:T(8,128)(2,1)S(1)}, u32[]{:S(2)}, u32[]{:S(2)}) %collective-permute-start.8) | collective-permute-done | bytes 155680 | tf_op jit(solution)/shard_map/ppermute | solution.py:381
  28.9 2.2 %collective-permute-start.12 = (s16[152,512]{1,0:T(8,128)(2,1)S(1)}, s16[152,512]{1,0:T(8,128)(2,1)S(1)}, u32[]{:S(2)}, u32[]{:S(2)}) collective-permute-start(s16[152,512]{1,0:T(8,128)(2,1)S(1)} %merge.4), channel_id=1, source_target_pairs={{0,2},{1,3},{2,0},{3,1},{4,6},{5,7},{6,4},{7,5},{8,10},{9,11},{10,... | collective-permute-start | bytes 466952 | tf_op jit(solution)/shard_map/ppermute | solution.py:381
  31.2 1.2 %collective-permute-start.9 = (s16[136,512]{1,0:T(8,128)(2,1)S(1)}, s16[136,512]{1,0:T(8,128)(2,1)S(1)}, u32[]{:S(2)}, u32[]{:S(2)}) collective-permute-start(s16[136,512]{1,0:T(8,128)(2,1)S(1)} %get-tuple-element.51), channel_id=1, source_target_pairs={{0,4},{1,5},{2,6},{3,7},{4,0},{5,1},{6,2},{7,3},{8,12},{9,13},{10,... | collective-permute-start | bytes 417800 | tf_op jit(solution)/shard_map/ppermute | solution.py:381
  33.2 1.3 %collective-permute-start.15 = (s16[120,512]{1,0:T(8,128)(2,1)S(1)}, s16[120,512]{1,0:T(8,128)(2,1)S(1)}, u32[]{:S(2)}, u32[]{:S(2)}) collective-permute-start(s16[120,512]{1,0:T(8,128)(2,1)S(1)} %get-tuple-element.68), channel_id=1, source_target_pairs={{0,8},{1,9},{2,10},{3,11},{4,12},{5,13},{6,14},{7,15},{8,0},{9,1},... | collective-permute-start | bytes 368648 | tf_op jit(solution)/shard_map/ppermute | solution.py:381
  34.5 1.4 %collective-permute-start.16 = (s16[120,512]{1,0:T(8,128)(2,1)S(1)}, s16[120,512]{1,0:T(8,128)(2,1)S(1)}, u32[]{:S(2)}, u32[]{:S(2)}) collective-permute-start(s16[120,512]{1,0:T(8,128)(2,1)S(1)} %get-tuple-element.54), channel_id=1, source_target_pairs={{0,12},{1,13},{2,14},{3,15},{4,8},{5,9},{6,10},{7,11},{8,4},{9,5},... | collective-permute-start | bytes 368648 | tf_op jit(solution)/shard_map/ppermute | solution.py:381
  35.9 4.5 %collective-permute-start.13 = (s16[152,512]{1,0:T(8,128)(2,1)S(1)}, s16[152,512]{1,0:T(8,128)(2,1)S(1)}, u32[]{:S(2)}, u32[]{:S(2)}) collective-permute-start(s16[152,512]{1,0:T(8,128)(2,1)S(1)} %collective-permute-done.12.refs_4_), channel_id=1, source_target_pairs={{0,16},{1,17},{4,20},{5,21},{8,24},{9,25},{12,28},{13,29},{18,2},{... | collective-permute-start | bytes 466952 | tf_op jit(solution)/shard_map/ppermute | solution.py:381
  40.5 1.3 %collective-permute-start.10 = (s16[136,512]{1,0:T(8,128)(2,1)S(1)}, s16[136,512]{1,0:T(8,128)(2,1)S(1)}, u32[]{:S(2)}, u32[]{:S(2)}) collective-permute-start(s16[136,512]{1,0:T(8,128)(2,1)S(1)} %get-tuple-element.61), channel_id=1, source_target_pairs={{2,18},{3,19},{6,22},{7,23},{10,26},{11,27},{14,30},{15,31},{16,0}... | collective-permute-start | bytes 417800 | tf_op jit(solution)/shard_map/ppermute | solution.py:381
  41.9 1.3 %collective-permute-start.11 = (s16[136,512]{1,0:T(8,128)(2,1)S(1)}, s16[136,512]{1,0:T(8,128)(2,1)S(1)}, u32[]{:S(2)}, u32[]{:S(2)}) collective-permute-start(s16[136,512]{1,0:T(8,128)(2,1)S(1)} %get-tuple-element.65), channel_id=1, source_target_pairs={{2,18},{3,19},{6,22},{7,23},{10,26},{11,27},{14,30},{15,31},{16,0}... | collective-permute-start | bytes 417800 | tf_op jit(solution)/shard_map/ppermute | solution.py:381
  44.1 8.2 %collective-permute-start.17 = (s16[120,512]{1,0:T(8,128)(2,1)S(1)}, s16[120,512]{1,0:T(8,128)(2,1)S(1)}, u32[]{:S(2)}, u32[]{:S(2)}) collective-permute-start(s16[120,512]{1,0:T(8,128)(2,1)S(1)} %merge.7), channel_id=1, source_target_pairs={{0,2},{1,3},{4,6},{5,7},{8,10},{9,11},{12,14},{13,15},{18,16},{19,... | collective-permute-start | bytes 368648 | tf_op jit(solution)/shard_map/ppermute | solution.py:381
  52.3 3.2 %collective-permute-done.17.refs_6_ = s16[120,512]{1,0:T(8,128)(2,1)S(1)} collective-permute-done((s16[120,512]{1,0:T(8,128)(2,1)S(1)}, s16[120,512]{1,0:T(8,128)(2,1)S(1)}, u32[]{:S(2)}, u32[]{:S(2)}) %collective-permute-start.17) | collective-permute-done | bytes 122912 | tf_op jit(solution)/shard_map/ppermute | solution.py:381
  55.4 1.1 %collective-permute-done.11.refs_3_ = s16[136,512]{1,0:T(8,128)(2,1)S(1)} collective-permute-done((s16[136,512]{1,0:T(8,128)(2,1)S(1)}, s16[136,512]{1,0:T(8,128)(2,1)S(1)}, u32[]{:S(2)}, u32[]{:S(2)}) %collective-permute-start.11) | collective-permute-done | bytes 139296 | tf_op jit(solution)/shard_map/ppermute | solution.py:381
  56.5 0.9 %finish.1 = bf16[256,512]{1,0:T(8,128)(2,1)} custom-call(f32[128,512]{1,0:T(8,128)S(1)} %get-tuple-element.60.refs_0_, f32[128,512]{1,0:T(8,128)S(1)} %get-tuple-element.64.refs_1_, s16[136,512]{1,0:T(8,128)(2,1)S(1)} %collective-permute-done.10.refs_2_, s16[136,512]{1,0:T(8,128)(2,1)S(1)} %collective-permute-done.11.refs_3_, ...), custom_call_target="tpu_custom_call" | custom-call | tf_op jit(solution)/shard_map/finish/pallas_call | solution.py:260
  (30 shorter events, 7.2 us)
Async XLA Ops:
  0.0 6.0 %collective-permute-start = (bf16[1536,1024]{1,0:T(8,128)(2,1)}, bf16[1536,1024]{1,0:T(8,128)(2,1)S(1)}, u32[]{:S(2)}, u32[]{:S(2)}) collective-permute-start(bf16[1536,1024]{1,0:T(8,128)(2,1)} %panels_in.1), channel_id=1, source_target_pairs={{0,1},{1,0},{2,3},{3,2},{4,5},{5,4},{6,7},{7,6},{8,9},{9,8},{10,11... | collective-permute-start | bytes 9437192 | tf_op jit(solution)/shard_map/ppermute | solution.py:381
  2.7 13.6 %collective-permute-start.2 = (bf16[144,1536]{1,0:T(8,128)(2,1)S(1)}, bf16[144,1536]{1,0:T(8,128)(2,1)S(1)}, u32[]{:S(2)}, u32[]{:S(2)}) collective-permute-start(bf16[144,1536]{1,0:T(8,128)(2,1)S(1)} %get-tuple-element.39), channel_id=1, source_target_pairs={{0,2},{1,3},{2,0},{3,1},{4,6},{5,7},{6,4},{7,5},{8,10},{9,11},{10,... | collective-permute-start | bytes 1327112 | tf_op jit(solution)/shard_map/ppermute | solution.py:381
  6.8 14.2 %collective-permute-start.1 = (s16[264,512]{1,0:T(8,128)(2,1)S(1)}, s16[264,512]{1,0:T(8,128)(2,1)S(1)}, u32[]{:S(2)}, u32[]{:S(2)}) collective-permute-start(s16[264,512]{1,0:T(8,128)(2,1)S(1)} %leaving.1), channel_id=1, source_target_pairs={{0,4},{1,5},{2,6},{3,7},{4,0},{5,1},{6,2},{7,3},{8,12},{9,13},{10,... | collective-permute-start | bytes 811016 | tf_op jit(solution)/shard_map/ppermute | solution.py:381
  10.4 10.7 %collective-permute-start.6 = (s16[136,1024]{1,0:T(8,128)(2,1)S(1)}, s16[136,1024]{1,0:T(8,128)(2,1)S(1)}, u32[]{:S(2)}, u32[]{:S(2)}) collective-permute-start(s16[136,1024]{1,0:T(8,128)(2,1)S(1)} %chosen.2), channel_id=1, source_target_pairs={{0,8},{1,9},{2,10},{3,11},{4,12},{5,13},{6,14},{7,15},{8,0},{9,1},... | collective-permute-start | bytes 835592 | tf_op jit(solution)/shard_map/ppermute | solution.py:381
  12.0 11.8 %collective-permute-start.5 = (bf16[112,1536]{1,0:T(8,128)(2,1)S(1)}, bf16[112,1536]{1,0:T(8,128)(2,1)S(1)}, u32[]{:S(2)}, u32[]{:S(2)}) collective-permute-start(bf16[112,1536]{1,0:T(8,128)(2,1)S(1)} %get-tuple-element.49), channel_id=1, source_target_pairs={{0,2},{1,3},{2,0},{3,1},{4,6},{5,7},{6,4},{7,5},{8,10},{9,11},{10,... | collective-permute-start | bytes 1032200 | tf_op jit(solution)/shard_map/ppermute | solution.py:381
  17.3 8.0 %collective-permute-start.4 = (s16[152,512]{1,0:T(8,128)(2,1)S(1)}, s16[152,512]{1,0:T(8,128)(2,1)S(1)}, u32[]{:S(2)}, u32[]{:S(2)}) collective-permute-start(s16[152,512]{1,0:T(8,128)(2,1)S(1)} %get-tuple-element.48), channel_id=1, source_target_pairs={{0,4},{1,5},{2,6},{3,7},{4,0},{5,1},{6,2},{7,3},{8,12},{9,13},{10,... | collective-permute-start | bytes 466952 | tf_op jit(solution)/shard_map/ppermute | solution.py:381
  19.4 6.9 %collective-permute-start.7 = (s16[152,512]{1,0:T(8,128)(2,1)S(1)}, s16[152,512]{1,0:T(8,128)(2,1)S(1)}, u32[]{:S(2)}, u32[]{:S(2)}) collective-permute-start(s16[152,512]{1,0:T(8,128)(2,1)S(1)} %get-tuple-element.57), channel_id=1, source_target_pairs={{0,8},{1,9},{2,10},{3,11},{4,12},{5,13},{6,14},{7,15},{8,0},{9,1},... | collective-permute-start | bytes 466952 | tf_op jit(solution)/shard_map/ppermute | solution.py:381
  20.9 7.8 %collective-permute-start.8 = (s16[152,512]{1,0:T(8,128)(2,1)S(1)}, s16[152,512]{1,0:T(8,128)(2,1)S(1)}, u32[]{:S(2)}, u32[]{:S(2)}) collective-permute-start(s16[152,512]{1,0:T(8,128)(2,1)S(1)} %get-tuple-element.45), channel_id=1, source_target_pairs={{0,12},{1,13},{2,14},{3,15},{4,8},{5,9},{6,10},{7,11},{8,4},{9,5},... | collective-permute-start | bytes 466952 | tf_op jit(solution)/shard_map/ppermute | solution.py:381
  21.1 13.4 %collective-permute-start.3 = (s16[136,512]{1,0:T(8,128)(2,1)S(1)}, s16[136,512]{1,0:T(8,128)(2,1)S(1)}, u32[]{:S(2)}, u32[]{:S(2)}) collective-permute-start(s16[136,512]{1,0:T(8,128)(2,1)S(1)} %get-tuple-element.47), channel_id=1, source_target_pairs={{0,8},{1,9},{2,10},{3,11},{4,12},{5,13},{6,14},{7,15},{8,0},{9,1},... | collective-permute-start | bytes 417800 | tf_op jit(solution)/shard_map/ppermute | solution.py:381
  28.9 6.9 %collective-permute-start.12 = (s16[152,512]{1,0:T(8,128)(2,1)S(1)}, s16[152,512]{1,0:T(8,128)(2,1)S(1)}, u32[]{:S(2)}, u32[]{:S(2)}) collective-permute-start(s16[152,512]{1,0:T(8,128)(2,1)S(1)} %merge.4), channel_id=1, source_target_pairs={{0,2},{1,3},{2,0},{3,1},{4,6},{5,7},{6,4},{7,5},{8,10},{9,11},{10,... | collective-permute-start | bytes 466952 | tf_op jit(solution)/shard_map/ppermute | solution.py:381
  31.2 9.3 %collective-permute-start.9 = (s16[136,512]{1,0:T(8,128)(2,1)S(1)}, s16[136,512]{1,0:T(8,128)(2,1)S(1)}, u32[]{:S(2)}, u32[]{:S(2)}) collective-permute-start(s16[136,512]{1,0:T(8,128)(2,1)S(1)} %get-tuple-element.51), channel_id=1, source_target_pairs={{0,4},{1,5},{2,6},{3,7},{4,0},{5,1},{6,2},{7,3},{8,12},{9,13},{10,... | collective-permute-start | bytes 417800 | tf_op jit(solution)/shard_map/ppermute | solution.py:381
  32.4 9.5 %collective-permute-start.14 = (s16[120,512]{1,0:T(8,128)(2,1)S(1)}, s16[120,512]{1,0:T(8,128)(2,1)S(1)}, u32[]{:S(2)}, u32[]{:S(2)}) collective-permute-start(s16[120,512]{1,0:T(8,128)(2,1)S(1)} %get-tuple-element.66), channel_id=1, source_target_pairs={{0,4},{1,5},{2,6},{3,7},{4,0},{5,1},{6,2},{7,3},{8,12},{9,13},{10,... | collective-permute-start | bytes 368648 | tf_op jit(solution)/shard_map/ppermute | solution.py:381
  33.2 10.0 %collective-permute-start.15 = (s16[120,512]{1,0:T(8,128)(2,1)S(1)}, s16[120,512]{1,0:T(8,128)(2,1)S(1)}, u32[]{:S(2)}, u32[]{:S(2)}) collective-permute-start(s16[120,512]{1,0:T(8,128)(2,1)S(1)} %get-tuple-element.68), channel_id=1, source_target_pairs={{0,8},{1,9},{2,10},{3,11},{4,12},{5,13},{6,14},{7,15},{8,0},{9,1},... | collective-permute-start | bytes 368648 | tf_op jit(solution)/shard_map/ppermute | solution.py:381
  34.5 8.7 %collective-permute-start.16 = (s16[120,512]{1,0:T(8,128)(2,1)S(1)}, s16[120,512]{1,0:T(8,128)(2,1)S(1)}, u32[]{:S(2)}, u32[]{:S(2)}) collective-permute-start(s16[120,512]{1,0:T(8,128)(2,1)S(1)} %get-tuple-element.54), channel_id=1, source_target_pairs={{0,12},{1,13},{2,14},{3,15},{4,8},{5,9},{6,10},{7,11},{8,4},{9,5},... | collective-permute-start | bytes 368648 | tf_op jit(solution)/shard_map/ppermute | solution.py:381
  35.9 20.6 %collective-permute-start.13 = (s16[152,512]{1,0:T(8,128)(2,1)S(1)}, s16[152,512]{1,0:T(8,128)(2,1)S(1)}, u32[]{:S(2)}, u32[]{:S(2)}) collective-permute-start(s16[152,512]{1,0:T(8,128)(2,1)S(1)} %collective-permute-done.12.refs_4_), channel_id=1, source_target_pairs={{0,16},{1,17},{4,20},{5,21},{8,24},{9,25},{12,28},{13,29},{18,2},{... | collective-permute-start | bytes 466952 | tf_op jit(solution)/shard_map/ppermute | solution.py:381
  40.5 14.9 %collective-permute-start.10 = (s16[136,512]{1,0:T(8,128)(2,1)S(1)}, s16[136,512]{1,0:T(8,128)(2,1)S(1)}, u32[]{:S(2)}, u32[]{:S(2)}) collective-permute-start(s16[136,512]{1,0:T(8,128)(2,1)S(1)} %get-tuple-element.61), channel_id=1, source_target_pairs={{2,18},{3,19},{6,22},{7,23},{10,26},{11,27},{14,30},{15,31},{16,0}... | collective-permute-start | bytes 417800 | tf_op jit(solution)/shard_map/ppermute | solution.py:381
  41.9 14.6 %collective-permute-start.11 = (s16[136,512]{1,0:T(8,128)(2,1)S(1)}, s16[136,512]{1,0:T(8,128)(2,1)S(1)}, u32[]{:S(2)}, u32[]{:S(2)}) collective-permute-start(s16[136,512]{1,0:T(8,128)(2,1)S(1)} %get-tuple-element.65), channel_id=1, source_target_pairs={{2,18},{3,19},{6,22},{7,23},{10,26},{11,27},{14,30},{15,31},{16,0}... | collective-permute-start | bytes 417800 | tf_op jit(solution)/shard_map/ppermute | solution.py:381
  43.4 8.9 %collective-permute-start.18 = (s16[120,512]{1,0:T(8,128)(2,1)S(1)}, s16[120,512]{1,0:T(8,128)(2,1)S(1)}, u32[]{:S(2)}, u32[]{:S(2)}) collective-permute-start(s16[120,512]{1,0:T(8,128)(2,1)S(1)} %merge.7), channel_id=1, source_target_pairs={{2,16},{3,17},{6,20},{7,21},{10,24},{11,25},{14,28},{15,29},{16,2}... | collective-permute-start | bytes 368648 | tf_op jit(solution)/shard_map/ppermute | solution.py:381
  44.1 11.3 %collective-permute-start.17 = (s16[120,512]{1,0:T(8,128)(2,1)S(1)}, s16[120,512]{1,0:T(8,128)(2,1)S(1)}, u32[]{:S(2)}, u32[]{:S(2)}) collective-permute-start(s16[120,512]{1,0:T(8,128)(2,1)S(1)} %merge.7), channel_id=1, source_target_pairs={{0,2},{1,3},{4,6},{5,7},{8,10},{9,11},{12,14},{13,15},{18,16},{19,... | collective-permute-start | bytes 368648 | tf_op jit(solution)/shard_map/ppermute | solution.py:381
where the time goes:
time: 57.7 us; the launch traced here: 57.4 us
  starting transfers between devices  37.7 us (65%)
  waiting for transfers between devices  9.9 us (17%)
  Pallas kernels  9.64 us (17%)
    ppermute x19, starting transfers between devices, permute(): return lax.ppermute(value, ('row', 'col'), pairs)  37.7 us
    ppermute x19, waiting for transfers between devices, permute(): return lax.ppermute(value, ('row', 'col'), pairs)  9.9 us
    pallas_call x4, Pallas kernels, quarters(): pl.pallas_call(functools.partial(quarter_kernel, coded=coded, spread=spre...  2.9 us
    pallas_call x1, Pallas kernels, build(): pl.pallas_call(build_kernel, out_shape=[jax.ShapeDtypeStruct((height, tal...  2.17 us
    pallas_call x2, Pallas kernels, products(): pl.pallas_call(functools.partial(product_kernel, count=len(blocks), coded...  1.41 us
    pallas_call x2, Pallas kernels, chosen(): pl.pallas_call(functools.partial(chosen_kernel, coded=coded, spread=sprea...  1.3 us
  transfers between devices with their start and end apart: 19, of which 6 were waited for; matrix products, arithmetic and copies ran while one was open for 0% of the time, Pallas kernels for 15%

commit v1 on v0

--- a/solution.py
+++ b/solution.py
@@ -80,10 +80,8 @@
     "stay_1",
     "code_0",
     "near_0",
-    "code_a",
-    "far_a",
-    "code_b",
-    "far_b",
+    "code_own",
+    "far_own",
     "far_0",
     "code_1",
     "near_1",
@@ -362,6 +360,27 @@
     )(coded, kept)
 
 
+def join_kernel(*refs):
+    count = (len(refs) - 2) // 2
+    value = jnp.concatenate(
+        [kept[...] + decode(coded[...], kept.shape[0]) for coded, kept in zip(refs[:count], refs[count:-2])], 0
+    )
+    refs[-2][...] = value
+    encode(value, refs[-1])
+
+
+def join(codeds, kepts):
+    height, half = sum(kept.shape[0] for kept in kepts), kepts[0].shape[1]
+    return pl.pallas_call(
+        join_kernel,
+        out_shape=[jax.ShapeDtypeStruct((height, half), jnp.float32), coded_shape(height, half)],
+        in_specs=[VMEM] * (2 * len(kepts)),
+        out_specs=[VMEM, VMEM],
+        compiler_params=SMALL,
+        name="join",
+    )(*codeds, *kepts)
+
+
 def after(value, *others):
     return lax.optimization_barrier((value, *others))[0]
 
@@ -459,12 +478,16 @@
             return (along if FIRST[name] == "x" else across)(done["split", name][k][1])
 
         def code(name, k):
+            if name == "own":
+                gots = [done["second", n][0] for n in OWN]
+                gots[0] = tied(gots[0])
+                return folded(*reversed(join(gots, [done["split", n][0][0] for n in OWN])))
             if FIRST[name] == "xz":
                 gots, hold = list(done["first", name][k]), done["stay", name][k]
             else:
                 gots, hold = [done["second", name][k]], done["split", name][k][0]
             gots[0] = tied(gots[0])
-            if inner or name in OWN:
+            if inner:
                 return folded(*reversed(merge(gots, hold, 1)))
             return merge(gots, hold, 0)
 
@@ -476,8 +499,8 @@
 
         def far(name, k):
             shift = last * spread
-            if name in OWN or name not in TURN:
-                m = 0 if name in OWN else moved[k]
+            if name == "own" or name not in TURN:
+                m = 0 if name == "own" else moved[k]
                 return permute(
                     done["code", name][k][1],
                     lambda r, c: (r ^ shift, c ^ m) if met(r, c, inner) and not met(r, c, last) else None,
@@ -503,9 +526,9 @@
         for k in range(len(moved)):
             for j in range(chunks):
                 parts += [done["near", f"{j}"][k], done["far", f"{j}"][k]]
-        kepts = [done["code", name][0][0] for name in OWN]
+        kept, arrived = done["code", "own"][0][0], done["far", "own"][0]
         heights = tuple(value.shape[0] for value in dense[0])
-        return finish(kepts, [done["far", name][0] for name in OWN], parts, heights, spread)
+        return finish([kept], [arrived], parts, heights, spread)
 
     return jax.shard_map(
         body,

time: 57.7 us -> 58.1 us (level)
  starting transfers between devices: 37.7 us -> 39.4 us
  waiting for transfers between devices: 9.9 us -> 8.73 us
    ppermute x19 -> x18, starting transfers between devices: 37.7 us -> 39.4 us  [permute(): return lax.ppermute(value, ('row', 'col'), pairs)]
    ppermute x19 -> x18, waiting for transfers between devices: 9.9 us -> 8.73 us  [permute(): return lax.ppermute(value, ('row', 'col'), pairs)]
  transfers between devices with their start and end apart: 19 -> 18, of which waited for: 6 -> 6; matrix products, arithmetic and copies ran while one was open for 0% -> 0% of each run, Pallas kernels for 15% -> 15%
where the time goes in v1:
time: 58.1 us; the launch traced here: 57.9 us
  starting transfers between devices  39.4 us (68%)
  Pallas kernels  9.59 us (17%)
  waiting for transfers between devices  8.73 us (15%)
    ppermute x18, starting transfers between devices, permute(): return lax.ppermute(value, ('row', 'col'), pairs)  39.4 us
    ppermute x18, waiting for transfers between devices, permute(): return lax.ppermute(value, ('row', 'col'), pairs)  8.73 us
    pallas_call x4, Pallas kernels, quarters(): pl.pallas_call(functools.partial(quarter_kernel, coded=coded, spread=spre...  2.89 us
    pallas_call x1, Pallas kernels, build(): pl.pallas_call(build_kernel, out_shape=[jax.ShapeDtypeStruct((height, tal...  2.17 us
    pallas_call x2, Pallas kernels, products(): pl.pallas_call(functools.partial(product_kernel, count=len(blocks), coded...  1.41 us
    pallas_call x2, Pallas kernels, chosen(): pl.pallas_call(functools.partial(chosen_kernel, coded=coded, spread=sprea...  1.3 us
  transfers between devices with their start and end apart: 18, of which 6 were waited for; matrix products, arithmetic and copies ran while one was open for 0% of the time, Pallas kernels for 15%

profile of v1, /device:TPU:0, one launch (start us, length us, event | category | flops | bytes accessed | tf_op | source)
XLA Modules:
  0.0 57.9 jit_solution(886223285069821179)
XLA Ops:
  0.5 2.2 %build.1 = (bf16[128,1536]{1,0:T(8,128)(2,1)S(1)}, bf16[128,1536]{1,0:T(8,128)(2,1)S(1)}, bf16[144,1536]{1,0:T(8,128)(2,1)S(1)}, bf16[112,1536]{1,0:T(8,128)(2,1)S(1)}, bf16[1536,1024]{1,0:T(8,128)(2,1)S(1)}) custom-call(s32[12]{0:T(128)} %bitcast.2, s32[24]{0:T(128)} %bitcast.3, bf16[24,128,128]{2,1,0:T(8,128)(2,1)} %tiles_in.1, bf16[1536,1024]{1,0:T(8,128)(2,1)} %panels_in.1), custom_call_target="tpu_custom_call" | custom-call | tf_op jit(solution)/shard_map/build/pallas_call | solution.py:137
  2.7 2.6 %collective-permute-start.2 = (bf16[144,1536]{1,0:T(8,128)(2,1)S(1)}, bf16[144,1536]{1,0:T(8,128)(2,1)S(1)}, u32[]{:S(2)}, u32[]{:S(2)}) collective-permute-start(bf16[144,1536]{1,0:T(8,128)(2,1)S(1)} %get-tuple-element.36), channel_id=1, source_target_pairs={{0,2},{1,3},{2,0},{3,1},{4,6},{5,7},{6,4},{7,5},{8,10},{9,11},{10,... | collective-permute-start | bytes 1327112 | tf_op jit(solution)/shard_map/ppermute | solution.py:400
  6.0 0.8 %leaving.1 = s16[264,512]{1,0:T(8,128)(2,1)S(1)} custom-call(bf16[128,1536]{1,0:T(8,128)(2,1)S(1)} %get-tuple-element.39.refs_0_, bf16[1536,1024]{1,0:T(8,128)(2,1)S(1)} %get-tuple-element.35.refs_1_.refs_0_.first, bf16[1536,1024]{1,0:T(8,128)(2,1)S(1)} %collective-permute-done.refs_2_.refs_1_.second), custom_call_target="tpu_custom_call" | custom-call | tf_op jit(solution)/shard_map/leaving/pallas_call | solution.py:178
  6.8 2.9 %collective-permute-start.1 = (s16[264,512]{1,0:T(8,128)(2,1)S(1)}, s16[264,512]{1,0:T(8,128)(2,1)S(1)}, u32[]{:S(2)}, u32[]{:S(2)}) collective-permute-start(s16[264,512]{1,0:T(8,128)(2,1)S(1)} %leaving.1), channel_id=1, source_target_pairs={{0,4},{1,5},{2,6},{3,7},{4,0},{5,1},{6,2},{7,3},{8,12},{9,13},{10,... | collective-permute-start | bytes 811016 | tf_op jit(solution)/shard_map/ppermute | solution.py:400
  9.7 0.7 %chosen.2 = s16[136,1024]{1,0:T(8,128)(2,1)S(1)} custom-call(bf16[128,1536]{1,0:T(8,128)(2,1)S(1)} %get-tuple-element.40.block, bf16[1536,1024]{1,0:T(8,128)(2,1)S(1)} %get-tuple-element.35.refs_1_.refs_0_.first, bf16[1536,1024]{1,0:T(8,128)(2,1)S(1)} %collective-permute-done.refs_2_.refs_1_.second), custom_call_target="tpu_custom_call" | custom-call | tf_op jit(solution)/shard_map/chosen/pallas_call | solution.py:288
  10.4 1.6 %collective-permute-start.6 = (s16[136,1024]{1,0:T(8,128)(2,1)S(1)}, s16[136,1024]{1,0:T(8,128)(2,1)S(1)}, u32[]{:S(2)}, u32[]{:S(2)}) collective-permute-start(s16[136,1024]{1,0:T(8,128)(2,1)S(1)} %chosen.2), channel_id=1, source_target_pairs={{0,8},{1,9},{2,10},{3,11},{4,12},{5,13},{6,14},{7,15},{8,0},{9,1},... | collective-permute-start | bytes 835592 | tf_op jit(solution)/shard_map/ppermute | solution.py:400
  13.3 3.0 %collective-permute-done.2.block = bf16[144,1536]{1,0:T(8,128)(2,1)S(1)} collective-permute-done((bf16[144,1536]{1,0:T(8,128)(2,1)S(1)}, bf16[144,1536]{1,0:T(8,128)(2,1)S(1)}, u32[]{:S(2)}, u32[]{:S(2)}) %collective-permute-start.2) | collective-permute-done | bytes 442400 | tf_op jit(solution)/shard_map/ppermute | solution.py:400
  16.3 1.0 %quarters.4 = (s16[152,512]{1,0:T(8,128)(2,1)S(1)}, s16[152,512]{1,0:T(8,128)(2,1)S(1)}, s16[152,512]{1,0:T(8,128)(2,1)S(1)}) custom-call(bf16[144,1536]{1,0:T(8,128)(2,1)S(1)} %collective-permute-done.2.block, bf16[1536,1024]{1,0:T(8,128)(2,1)S(1)} %get-tuple-element.35.refs_1_.refs_0_.first, bf16[1536,1024]{1,0:T(8,128)(2,1)S(1)} %collective-permute-done.refs_2_.refs_1_.second), custom_call_target="tpu_custom_call" | custom-call | tf_op jit(solution)/shard_map/quarters/pallas_call | solution.py:328
  17.3 2.1 %collective-permute-start.4 = (s16[152,512]{1,0:T(8,128)(2,1)S(1)}, s16[152,512]{1,0:T(8,128)(2,1)S(1)}, u32[]{:S(2)}, u32[]{:S(2)}) collective-permute-start(s16[152,512]{1,0:T(8,128)(2,1)S(1)} %get-tuple-element.45), channel_id=1, source_target_pairs={{0,4},{1,5},{2,6},{3,7},{4,0},{5,1},{6,2},{7,3},{8,12},{9,13},{10,... | collective-permute-start | bytes 466952 | tf_op jit(solution)/shard_map/ppermute | solution.py:400
  19.4 1.6 %collective-permute-start.7 = (s16[152,512]{1,0:T(8,128)(2,1)S(1)}, s16[152,512]{1,0:T(8,128)(2,1)S(1)}, u32[]{:S(2)}, u32[]{:S(2)}) collective-permute-start(s16[152,512]{1,0:T(8,128)(2,1)S(1)} %get-tuple-element.54), channel_id=1, source_target_pairs={{0,8},{1,9},{2,10},{3,11},{4,12},{5,13},{6,14},{7,15},{8,0},{9,1},... | collective-permute-start | bytes 466952 | tf_op jit(solution)/shard_map/ppermute | solution.py:400
  21.1 2.1 %collective-permute-start.3 = (s16[136,512]{1,0:T(8,128)(2,1)S(1)}, s16[136,512]{1,0:T(8,128)(2,1)S(1)}, u32[]{:S(2)}, u32[]{:S(2)}) collective-permute-start(s16[136,512]{1,0:T(8,128)(2,1)S(1)} %get-tuple-element.44), channel_id=1, source_target_pairs={{0,8},{1,9},{2,10},{3,11},{4,12},{5,13},{6,14},{7,15},{8,0},{9,1},... | collective-permute-start | bytes 417800 | tf_op jit(solution)/shard_map/ppermute | solution.py:400
  23.5 1.7 %collective-permute-start.9 = (s16[136,512]{1,0:T(8,128)(2,1)S(1)}, s16[136,512]{1,0:T(8,128)(2,1)S(1)}, u32[]{:S(2)}, u32[]{:S(2)}) collective-permute-start(s16[136,512]{1,0:T(8,128)(2,1)S(1)} %get-tuple-element.48), channel_id=1, source_target_pairs={{0,4},{1,5},{2,6},{3,7},{4,0},{5,1},{6,2},{7,3},{8,12},{9,13},{10,... | collective-permute-start | bytes 417800 | tf_op jit(solution)/shard_map/ppermute | solution.py:400
  25.6 1.0 %quarters.6 = (s16[120,512]{1,0:T(8,128)(2,1)S(1)}, s16[120,512]{1,0:T(8,128)(2,1)S(1)}, s16[120,512]{1,0:T(8,128)(2,1)S(1)}) custom-call(bf16[112,1536]{1,0:T(8,128)(2,1)S(1)} %collective-permute-done.5.block, bf16[1536,1024]{1,0:T(8,128)(2,1)S(1)} %get-tuple-element.35.refs_1_.refs_0_.first, bf16[1536,1024]{1,0:T(8,128)(2,1)S(1)} %collective-permute-done.refs_2_.refs_1_.second), custom_call_target="tpu_custom_call" | custom-call | tf_op jit(solution)/shard_map/quarters/pallas_call | solution.py:328
  27.1 1.7 %collective-permute-done.8.refs_2_ = s16[152,512]{1,0:T(8,128)(2,1)S(1)} collective-permute-done((s16[152,512]{1,0:T(8,128)(2,1)S(1)}, s16[152,512]{1,0:T(8,128)(2,1)S(1)}, u32[]{:S(2)}, u32[]{:S(2)}) %collective-permute-start.8) | collective-permute-done | bytes 155680 | tf_op jit(solution)/shard_map/ppermute | solution.py:400
  28.9 2.2 %collective-permute-start.11 = (s16[152,512]{1,0:T(8,128)(2,1)S(1)}, s16[152,512]{1,0:T(8,128)(2,1)S(1)}, u32[]{:S(2)}, u32[]{:S(2)}) collective-permute-start(s16[152,512]{1,0:T(8,128)(2,1)S(1)} %merge.2), channel_id=1, source_target_pairs={{0,2},{1,3},{2,0},{3,1},{4,6},{5,7},{6,4},{7,5},{8,10},{9,11},{10,... | collective-permute-start | bytes 466952 | tf_op jit(solution)/shard_map/ppermute | solution.py:400
  31.4 1.3 %collective-permute-start.10 = (s16[264,512]{1,0:T(8,128)(2,1)S(1)}, s16[264,512]{1,0:T(8,128)(2,1)S(1)}, u32[]{:S(2)}, u32[]{:S(2)}) collective-permute-start(s16[264,512]{1,0:T(8,128)(2,1)S(1)} %get-tuple-element.59), channel_id=1, source_target_pairs={{2,18},{3,19},{6,22},{7,23},{10,26},{11,27},{14,30},{15,31},{16,0}... | collective-permute-start | bytes 811016 | tf_op jit(solution)/shard_map/ppermute | solution.py:400
  32.7 1.3 %collective-permute-start.13 = (s16[120,512]{1,0:T(8,128)(2,1)S(1)}, s16[120,512]{1,0:T(8,128)(2,1)S(1)}, u32[]{:S(2)}, u32[]{:S(2)}) collective-permute-start(s16[120,512]{1,0:T(8,128)(2,1)S(1)} %get-tuple-element.60), channel_id=1, source_target_pairs={{0,4},{1,5},{2,6},{3,7},{4,0},{5,1},{6,2},{7,3},{8,12},{9,13},{10,... | collective-permute-start | bytes 368648 | tf_op jit(solution)/shard_map/ppermute | solution.py:400
  33.9 1.6 %collective-permute-start.14 = (s16[120,512]{1,0:T(8,128)(2,1)S(1)}, s16[120,512]{1,0:T(8,128)(2,1)S(1)}, u32[]{:S(2)}, u32[]{:S(2)}) collective-permute-start(s16[120,512]{1,0:T(8,128)(2,1)S(1)} %get-tuple-element.62), channel_id=1, source_target_pairs={{0,8},{1,9},{2,10},{3,11},{4,12},{5,13},{6,14},{7,15},{8,0},{9,1},... | collective-permute-start | bytes 368648 | tf_op jit(solution)/shard_map/ppermute | solution.py:400
  35.5 0.7 %collective-permute-start.15 = (s16[120,512]{1,0:T(8,128)(2,1)S(1)}, s16[120,512]{1,0:T(8,128)(2,1)S(1)}, u32[]{:S(2)}, u32[]{:S(2)}) collective-permute-start(s16[120,512]{1,0:T(8,128)(2,1)S(1)} %get-tuple-element.51), channel_id=1, source_target_pairs={{0,12},{1,13},{2,14},{3,15},{4,8},{5,9},{6,10},{7,11},{8,4},{9,5},... | collective-permute-start | bytes 368648 | tf_op jit(solution)/shard_map/ppermute | solution.py:400
  36.2 5.5 %collective-permute-start.12 = (s16[152,512]{1,0:T(8,128)(2,1)S(1)}, s16[152,512]{1,0:T(8,128)(2,1)S(1)}, u32[]{:S(2)}, u32[]{:S(2)}) collective-permute-start(s16[152,512]{1,0:T(8,128)(2,1)S(1)} %collective-permute-done.11.refs_2_), channel_id=1, source_target_pairs={{0,16},{1,17},{4,20},{5,21},{8,24},{9,25},{12,28},{13,29},{18,2},{... | collective-permute-start | bytes 466952 | tf_op jit(solution)/shard_map/ppermute | solution.py:400
  41.7 0.9 %collective-permute-done.15.refs_2_ = s16[120,512]{1,0:T(8,128)(2,1)S(1)} collective-permute-done((s16[120,512]{1,0:T(8,128)(2,1)S(1)}, s16[120,512]{1,0:T(8,128)(2,1)S(1)}, u32[]{:S(2)}, u32[]{:S(2)}) %collective-permute-start.15) | collective-permute-done | bytes 122912 | tf_op jit(solution)/shard_map/ppermute | solution.py:400
  43.5 11.1 %collective-permute-start.16 = (s16[120,512]{1,0:T(8,128)(2,1)S(1)}, s16[120,512]{1,0:T(8,128)(2,1)S(1)}, u32[]{:S(2)}, u32[]{:S(2)}) collective-permute-start(s16[120,512]{1,0:T(8,128)(2,1)S(1)} %merge.3), channel_id=1, source_target_pairs={{0,2},{1,3},{4,6},{5,7},{8,10},{9,11},{12,14},{13,15},{18,16},{19,... | collective-permute-start | bytes 368648 | tf_op jit(solution)/shard_map/ppermute | solution.py:400
  54.5 2.4 %collective-permute-done.16.refs_4_ = s16[120,512]{1,0:T(8,128)(2,1)S(1)} collective-permute-done((s16[120,512]{1,0:T(8,128)(2,1)S(1)}, s16[120,512]{1,0:T(8,128)(2,1)S(1)}, u32[]{:S(2)}, u32[]{:S(2)}) %collective-permute-start.16) | collective-permute-done | bytes 122912 | tf_op jit(solution)/shard_map/ppermute | solution.py:400
  56.9 0.9 %finish.1 = bf16[256,512]{1,0:T(8,128)(2,1)} custom-call(f32[256,512]{1,0:T(8,128)S(1)} %get-tuple-element.58.refs_0_, s16[264,512]{1,0:T(8,128)(2,1)S(1)} %collective-permute-done.10.refs_1_, s16[152,512]{1,0:T(8,128)(2,1)S(1)} %collective-permute-done.11.refs_2_, s16[152,512]{1,0:T(8,128)(2,1)S(1)} %collective-permute-done.12.refs_3_, ...), custom_call_target="tpu_custom_call" | custom-call | tf_op jit(solution)/shard_map/finish/pallas_call | solution.py:258
  (27 shorter events, 5.0 us)
Async XLA Ops:
  0.0 6.0 %collective-permute-start = (bf16[1536,1024]{1,0:T(8,128)(2,1)}, bf16[1536,1024]{1,0:T(8,128)(2,1)S(1)}, u32[]{:S(2)}, u32[]{:S(2)}) collective-permute-start(bf16[1536,1024]{1,0:T(8,128)(2,1)} %panels_in.1), channel_id=1, source_target_pairs={{0,1},{1,0},{2,3},{3,2},{4,5},{5,4},{6,7},{7,6},{8,9},{9,8},{10,11... | collective-permute-start | bytes 9437192 | tf_op jit(solution)/shard_map/ppermute | solution.py:400
  2.7 13.6 %collective-permute-start.2 = (bf16[144,1536]{1,0:T(8,128)(2,1)S(1)}, bf16[144,1536]{1,0:T(8,128)(2,1)S(1)}, u32[]{:S(2)}, u32[]{:S(2)}) collective-permute-start(bf16[144,1536]{1,0:T(8,128)(2,1)S(1)} %get-tuple-element.36), channel_id=1, source_target_pairs={{0,2},{1,3},{2,0},{3,1},{4,6},{5,7},{6,4},{7,5},{8,10},{9,11},{10,... | collective-permute-start | bytes 1327112 | tf_op jit(solution)/shard_map/ppermute | solution.py:400
  5.2 18.2 %collective-permute-start.5 = (bf16[112,1536]{1,0:T(8,128)(2,1)S(1)}, bf16[112,1536]{1,0:T(8,128)(2,1)S(1)}, u32[]{:S(2)}, u32[]{:S(2)}) collective-permute-start(bf16[112,1536]{1,0:T(8,128)(2,1)S(1)} %get-tuple-element.46), channel_id=1, source_target_pairs={{0,2},{1,3},{2,0},{3,1},{4,6},{5,7},{6,4},{7,5},{8,10},{9,11},{10,... | collective-permute-start | bytes 1032200 | tf_op jit(solution)/shard_map/ppermute | solution.py:400
  6.8 14.2 %collective-permute-start.1 = (s16[264,512]{1,0:T(8,128)(2,1)S(1)}, s16[264,512]{1,0:T(8,128)(2,1)S(1)}, u32[]{:S(2)}, u32[]{:S(2)}) collective-permute-start(s16[264,512]{1,0:T(8,128)(2,1)S(1)} %leaving.1), channel_id=1, source_target_pairs={{0,4},{1,5},{2,6},{3,7},{4,0},{5,1},{6,2},{7,3},{8,12},{9,13},{10,... | collective-permute-start | bytes 811016 | tf_op jit(solution)/shard_map/ppermute | solution.py:400
  10.4 10.7 %collective-permute-start.6 = (s16[136,1024]{1,0:T(8,128)(2,1)S(1)}, s16[136,1024]{1,0:T(8,128)(2,1)S(1)}, u32[]{:S(2)}, u32[]{:S(2)}) collective-permute-start(s16[136,1024]{1,0:T(8,128)(2,1)S(1)} %chosen.2), channel_id=1, source_target_pairs={{0,8},{1,9},{2,10},{3,11},{4,12},{5,13},{6,14},{7,15},{8,0},{9,1},... | collective-permute-start | bytes 835592 | tf_op jit(solution)/shard_map/ppermute | solution.py:400
  17.3 9.8 %collective-permute-start.4 = (s16[152,512]{1,0:T(8,128)(2,1)S(1)}, s16[152,512]{1,0:T(8,128)(2,1)S(1)}, u32[]{:S(2)}, u32[]{:S(2)}) collective-permute-start(s16[152,512]{1,0:T(8,128)(2,1)S(1)} %get-tuple-element.45), channel_id=1, source_target_pairs={{0,4},{1,5},{2,6},{3,7},{4,0},{5,1},{6,2},{7,3},{8,12},{9,13},{10,... | collective-permute-start | bytes 466952 | tf_op jit(solution)/shard_map/ppermute | solution.py:400
  19.4 7.7 %collective-permute-start.7 = (s16[152,512]{1,0:T(8,128)(2,1)S(1)}, s16[152,512]{1,0:T(8,128)(2,1)S(1)}, u32[]{:S(2)}, u32[]{:S(2)}) collective-permute-start(s16[152,512]{1,0:T(8,128)(2,1)S(1)} %get-tuple-element.54), channel_id=1, source_target_pairs={{0,8},{1,9},{2,10},{3,11},{4,12},{5,13},{6,14},{7,15},{8,0},{9,1},... | collective-permute-start | bytes 466952 | tf_op jit(solution)/shard_map/ppermute | solution.py:400
  20.9 7.8 %collective-permute-start.8 = (s16[152,512]{1,0:T(8,128)(2,1)S(1)}, s16[152,512]{1,0:T(8,128)(2,1)S(1)}, u32[]{:S(2)}, u32[]{:S(2)}) collective-permute-start(s16[152,512]{1,0:T(8,128)(2,1)S(1)} %get-tuple-element.42), channel_id=1, source_target_pairs={{0,12},{1,13},{2,14},{3,15},{4,8},{5,9},{6,10},{7,11},{8,4},{9,5},... | collective-permute-start | bytes 466952 | tf_op jit(solution)/shard_map/ppermute | solution.py:400
  21.1 10.1 %collective-permute-start.3 = (s16[136,512]{1,0:T(8,128)(2,1)S(1)}, s16[136,512]{1,0:T(8,128)(2,1)S(1)}, u32[]{:S(2)}, u32[]{:S(2)}) collective-permute-start(s16[136,512]{1,0:T(8,128)(2,1)S(1)} %get-tuple-element.44), channel_id=1, source_target_pairs={{0,8},{1,9},{2,10},{3,11},{4,12},{5,13},{6,14},{7,15},{8,0},{9,1},... | collective-permute-start | bytes 417800 | tf_op jit(solution)/shard_map/ppermute | solution.py:400
  23.5 7.7 %collective-permute-start.9 = (s16[136,512]{1,0:T(8,128)(2,1)S(1)}, s16[136,512]{1,0:T(8,128)(2,1)S(1)}, u32[]{:S(2)}, u32[]{:S(2)}) collective-permute-start(s16[136,512]{1,0:T(8,128)(2,1)S(1)} %get-tuple-element.48), channel_id=1, source_target_pairs={{0,4},{1,5},{2,6},{3,7},{4,0},{5,1},{6,2},{7,3},{8,12},{9,13},{10,... | collective-permute-start | bytes 417800 | tf_op jit(solution)/shard_map/ppermute | solution.py:400
  28.9 7.3 %collective-permute-start.11 = (s16[152,512]{1,0:T(8,128)(2,1)S(1)}, s16[152,512]{1,0:T(8,128)(2,1)S(1)}, u32[]{:S(2)}, u32[]{:S(2)}) collective-permute-start(s16[152,512]{1,0:T(8,128)(2,1)S(1)} %merge.2), channel_id=1, source_target_pairs={{0,2},{1,3},{2,0},{3,1},{4,6},{5,7},{6,4},{7,5},{8,10},{9,11},{10,... | collective-permute-start | bytes 466952 | tf_op jit(solution)/shard_map/ppermute | solution.py:400
  31.4 25.6 %collective-permute-start.10 = (s16[264,512]{1,0:T(8,128)(2,1)S(1)}, s16[264,512]{1,0:T(8,128)(2,1)S(1)}, u32[]{:S(2)}, u32[]{:S(2)}) collective-permute-start(s16[264,512]{1,0:T(8,128)(2,1)S(1)} %get-tuple-element.59), channel_id=1, source_target_pairs={{2,18},{3,19},{6,22},{7,23},{10,26},{11,27},{14,30},{15,31},{16,0}... | collective-permute-start | bytes 811016 | tf_op jit(solution)/shard_map/ppermute | solution.py:400
  32.7 9.0 %collective-permute-start.13 = (s16[120,512]{1,0:T(8,128)(2,1)S(1)}, s16[120,512]{1,0:T(8,128)(2,1)S(1)}, u32[]{:S(2)}, u32[]{:S(2)}) collective-permute-start(s16[120,512]{1,0:T(8,128)(2,1)S(1)} %get-tuple-element.60), channel_id=1, source_target_pairs={{0,4},{1,5},{2,6},{3,7},{4,0},{5,1},{6,2},{7,3},{8,12},{9,13},{10,... | collective-permute-start | bytes 368648 | tf_op jit(solution)/shard_map/ppermute | solution.py:400
  33.9 7.8 %collective-permute-start.14 = (s16[120,512]{1,0:T(8,128)(2,1)S(1)}, s16[120,512]{1,0:T(8,128)(2,1)S(1)}, u32[]{:S(2)}, u32[]{:S(2)}) collective-permute-start(s16[120,512]{1,0:T(8,128)(2,1)S(1)} %get-tuple-element.62), channel_id=1, source_target_pairs={{0,8},{1,9},{2,10},{3,11},{4,12},{5,13},{6,14},{7,15},{8,0},{9,1},... | collective-permute-start | bytes 368648 | tf_op jit(solution)/shard_map/ppermute | solution.py:400
  35.5 7.1 %collective-permute-start.15 = (s16[120,512]{1,0:T(8,128)(2,1)S(1)}, s16[120,512]{1,0:T(8,128)(2,1)S(1)}, u32[]{:S(2)}, u32[]{:S(2)}) collective-permute-start(s16[120,512]{1,0:T(8,128)(2,1)S(1)} %get-tuple-element.51), channel_id=1, source_target_pairs={{0,12},{1,13},{2,14},{3,15},{4,8},{5,9},{6,10},{7,11},{8,4},{9,5},... | collective-permute-start | bytes 368648 | tf_op jit(solution)/shard_map/ppermute | solution.py:400
  36.2 20.7 %collective-permute-start.12 = (s16[152,512]{1,0:T(8,128)(2,1)S(1)}, s16[152,512]{1,0:T(8,128)(2,1)S(1)}, u32[]{:S(2)}, u32[]{:S(2)}) collective-permute-start(s16[152,512]{1,0:T(8,128)(2,1)S(1)} %collective-permute-done.11.refs_2_), channel_id=1, source_target_pairs={{0,16},{1,17},{4,20},{5,21},{8,24},{9,25},{12,28},{13,29},{18,2},{... | collective-permute-start | bytes 466952 | tf_op jit(solution)/shard_map/ppermute | solution.py:400
  42.8 11.7 %collective-permute-start.17 = (s16[120,512]{1,0:T(8,128)(2,1)S(1)}, s16[120,512]{1,0:T(8,128)(2,1)S(1)}, u32[]{:S(2)}, u32[]{:S(2)}) collective-permute-start(s16[120,512]{1,0:T(8,128)(2,1)S(1)} %merge.3), channel_id=1, source_target_pairs={{2,16},{3,17},{6,20},{7,21},{10,24},{11,25},{14,28},{15,29},{16,2}... | collective-permute-start | bytes 368648 | tf_op jit(solution)/shard_map/ppermute | solution.py:400
  43.5 13.5 %collective-permute-start.16 = (s16[120,512]{1,0:T(8,128)(2,1)S(1)}, s16[120,512]{1,0:T(8,128)(2,1)S(1)}, u32[]{:S(2)}, u32[]{:S(2)}) collective-permute-start(s16[120,512]{1,0:T(8,128)(2,1)S(1)} %merge.3), channel_id=1, source_target_pairs={{0,2},{1,3},{4,6},{5,7},{8,10},{9,11},{12,14},{13,15},{18,16},{19,... | collective-permute-start | bytes 368648 | tf_op jit(solution)/shard_map/ppermute | solution.py:400
